TPU v7x, 32 devices: a whole 2x2x4 slice. The times are simulated.
32 devices in a mesh: space: 16 (over z, y, core), peer: 2 (over x).
Axes of the slice: x: 2, y: 2, z: 4, core: 2. Of those that a mesh axis runs over, the one named last changes fastest.
Arguments:
- wavefield: float32 [2, 9, 128, 64, 128], P('peer', None, 'space'), may hold values from -100 to 100
- buoyancy: float32 [128, 64, 128], P('space'), may hold values from 0.2 to 0.5
- lame_lambda: float32 [128, 64, 128], P('space'), may hold values from 0.06 to 0.12
- shear_modulus: float32 [128, 64, 128], P('space'), may hold values from 0.05 to 0.1
- scale_exponents: int32 [9, 16, 8, 16], P(None, 'space'), may hold values from -2 to 2
- source_cells: int32 [2, 8], replicated, may hold values from 0 to 1048575
- wavelet: float32 [2, 3, 8], replicated, may hold values from -18 to 18
Outputs:
- final_field: float32 [2, 9, 128, 64, 128], P('peer', None, 'space')
- stored: bfloat16 [2, 3, 9, 128, 64, 128], P('peer', None, None, 'space')
- statistics: float32 [2, 3, 2], P('peer')
All inputs are finite; a program needn't handle non-finite values.
Results may differ from a plain program's by a relative error of at most 0.0045.
Values may be sent and summed in bfloat16 or wider, within the bound.
A program may use at most 64 MiB of HBM per device.

v0:
```python
import jax
import jax.numpy as jnp
from jax import lax
from jax.sharding import PartitionSpec as P

BLOCK = 8
STEPS = 3


stencil_reach = 2
stencil_weights = (9.0 / 8.0, -1.0 / 24.0)
clip_level = 4.0
energy_floor = 1e-06


def extended(cells, sides, width):
    for axis, dim in sides:
        count = lax.axis_size(axis)
        ends = count - 1
        head = lax.slice_in_dim(cells, 0, width, axis=dim)
        tail = lax.slice_in_dim(cells, cells.shape[dim] - width, cells.shape[dim], axis=dim)
        cells = jnp.concatenate(
            [
                lax.ppermute(tail, axis, [(i, (i + 1) % count) for i in range(ends)]),
                cells,
                lax.ppermute(head, axis, [((i + 1) % count, i) for i in range(ends)]),
            ],
            axis=dim,
        )
    return cells


def from_partner(block, axis, bit):
    count = lax.axis_size(axis)
    route = []
    for low in range(count):
        high = low | 1 << bit
        if high != low and high < count:
            route += [(low, high), (high, low)]
    return lax.ppermute(block, axis, route)


def pad_along(values, dimension):
    widths = [(0, 0)] * values.ndim
    widths[dimension] = (stencil_reach, stencil_reach)
    return jnp.pad(values, widths)


def derivative(padded, dimension, forward):
    length = padded.shape[dimension] - 2 * stencil_reach
    summed = None
    for offset in range(1, stencil_reach + 1):
        weight = stencil_weights[offset - 1]
        if forward:
            above_at = stencil_reach + offset
            below_at = stencil_reach + 1 - offset
        else:
            above_at = stencil_reach + offset - 1
            below_at = stencil_reach - offset
        portion = weight * (
            lax.slice_in_dim(padded, above_at, above_at + length, axis=dimension)
            - lax.slice_in_dim(padded, below_at, below_at + length, axis=dimension)
        )
        summed = portion if summed is None else summed + portion
    return summed


def differ(values, dimension, forward):
    return derivative(pad_along(values, dimension), dimension, forward)


def advance(current, buoyancy, lame_lambda, shear_modulus, images, stress_padder, velocity_padder):
    velocity = [current[:, component] for component in range(3)]
    stress = [current[:, component] for component in range(3, 9)]
    depth_rims = stress_padder(current[:, 6:9])
    velocity[0] = velocity[0] + buoyancy * (
        differ(stress[0], 3, True)
        + differ(stress[2], 2, False)
        + derivative(depth_rims[:, 1], 1, False)
    )
    velocity[1] = velocity[1] + buoyancy * (
        differ(stress[2], 3, False)
        + differ(stress[1], 2, True)
        + derivative(depth_rims[:, 2], 1, False)
    )
    velocity[2] = velocity[2] + buoyancy * (
        differ(stress[4], 3, False)
        + differ(stress[5], 2, False)
        + derivative(depth_rims[:, 0], 1, True)
    )
    depth_rims = velocity_padder(jnp.stack(velocity, axis=1))
    strain = [
        differ(velocity[0], 3, False),
        differ(velocity[1], 2, False),
        derivative(depth_rims[:, 2], 1, False),
    ]
    dilation = strain[0] + strain[1] + strain[2]
    pressure = lame_lambda * dilation + images
    stress[0] = stress[0] + pressure + 2.0 * shear_modulus * strain[0]
    stress[1] = stress[1] + pressure + 2.0 * shear_modulus * strain[1]
    stress[3] = stress[3] + pressure + 2.0 * shear_modulus * strain[2]
    stress[2] = stress[2] + shear_modulus * (
        differ(velocity[0], 2, True) + differ(velocity[1], 3, True)
    )
    stress[4] = stress[4] + shear_modulus * (
        derivative(depth_rims[:, 0], 1, True) + differ(velocity[2], 3, True)
    )
    stress[5] = stress[5] + shear_modulus * (
        derivative(depth_rims[:, 1], 1, True) + differ(velocity[2], 2, True)
    )
    return jnp.stack(velocity + stress, axis=1)


def scale_tables(exponents):
    expanded = jnp.repeat(
        jnp.repeat(jnp.repeat(exponents, BLOCK, axis=1), BLOCK, axis=2), BLOCK, axis=3
    )
    upscale = jnp.zeros(expanded.shape, jnp.float32)
    downscale = jnp.zeros(expanded.shape, jnp.float32)
    for exponent in range(-2, 3):
        chosen = expanded == exponent
        upscale = jnp.where(chosen, jnp.float32(2.0**exponent), upscale)
        downscale = jnp.where(chosen, jnp.float32(2.0 ** (-exponent)), downscale)
    return (upscale, downscale)


def compress(current, upscale, downscale):
    payload = jnp.clip(current * downscale, -clip_level, clip_level).astype(jnp.bfloat16)
    levels = lax.optimization_barrier(payload).astype(jnp.float32)
    return (payload, levels, levels * upscale)


def finish(sums, cell_count):
    mean_size = sums[..., 0] / cell_count
    relative = sums[..., 1] / cell_count / (sums[..., 2] / cell_count + energy_floor)
    return jnp.stack([mean_size, jnp.sqrt(relative)], axis=-1)


def per_device(
    wavefield, buoyancy, lame_lambda, shear_modulus, scale_exponents, source_cells, wavelet
):
    peer_rank = lax.axis_index("peer")
    slab_rank = lax.axis_index("space")
    depth_cells = wavefield.shape[2]
    row_count = wavefield.shape[3]
    columns = wavefield.shape[4]
    slab_size = depth_cells * row_count * columns
    cell_count = 9 * slab_size * lax.axis_size("space")
    upscale, downscale = scale_tables(scale_exponents)

    def stress_padder(stack):
        return extended(stack.astype(jnp.bfloat16), (("space", 2),), stencil_reach).astype(
            stack.dtype
        )

    def velocity_padder(stack):
        return extended(stack.astype(jnp.bfloat16), (("space", 2),), stencil_reach).astype(
            stack.dtype
        )

    def local_sources(shot_index, instant):
        local_index = source_cells[shot_index] - slab_rank * slab_size
        inside = (local_index >= 0) & (local_index < slab_size)
        placed = jnp.where(inside, local_index, slab_size)
        flat = (
            jnp.zeros((slab_size,), jnp.float32)
            .at[placed]
            .add(wavelet[shot_index, instant], mode="drop")
        )
        return flat.reshape(depth_cells, row_count, columns)

    current = wavefield
    shot_list = [peer_rank]
    stored_list = []
    local_sums = []
    for instant in range(STEPS):
        images = jnp.stack([local_sources(shot_index, instant) for shot_index in shot_list], axis=0)
        current = advance(
            current, buoyancy, lame_lambda, shear_modulus, images, stress_padder, velocity_padder
        )
        payload, levels, restored = compress(current, upscale, downscale)
        stored_list.append(from_partner(payload, "peer", 0)[0])
        misfit = current[0] - restored[0]
        step_terms = jnp.stack(
            [
                jnp.sum(jnp.abs(levels[0])),
                jnp.sum(misfit * misfit),
                jnp.sum(current[0] * current[0]),
            ]
        )
        local_sums.append(step_terms)
    totals = lax.psum(jnp.stack(local_sums, axis=0), "space")
    statistics = finish(totals, cell_count)[None]
    stored = jnp.stack(stored_list, axis=0)[None]
    return (current, stored, statistics)


def solution(mesh):
    return jax.shard_map(
        per_device,
        mesh=mesh,
        in_specs=(
            P("peer", None, "space", None, None),
            P("space", None, None),
            P("space", None, None),
            P("space", None, None),
            P(None, "space", None, None),
            P(),
            P(),
        ),
        out_specs=(
            P("peer", None, "space", None, None),
            P("peer", None, None, "space", None, None),
            P("peer", None, None),
        ),
        check_vma=False,
    )
```

profile of v0, /device:TPU:9, one launch (start us, length us, event | category | flops | bytes accessed | tf_op | source)
XLA Modules:
  0.0 169.8 jit_solution(6454450619774466129)
XLA Ops:
  0.6 2.0 %convert.93 = bf16[1,9,8,64,128]{4,3,2,1,0:T(8,128)(2,1)S(1)} convert(f32[1,9,8,64,128]{4,3,2,1,0:T(8,128)} %param.7) | non-fusion elementwise | flops 589824 | bytes 3538944 | tf_op jit(solution)/shard_map/convert.30
  3.4 3.7 %collective-permute-start = (bf16[1,3,2,64,128]{4,3,2,1,0:T(8,128)(2,1)}, bf16[1,3,2,64,128]{4,3,2,1,0:T(8,128)(2,1)}, u32[]{:S(2)}, u32[]{:S(2)}) collective-permute-start(bf16[1,3,2,64,128]{4,3,2,1,0:T(8,128)(2,1)} %get-tuple-element.95), channel_id=1, source_target_pairs={{0,2},{2,4},{4,6},{6,8},{8,10},{10,12},{12,14},{14,16},{16,18},{18... | collective-permute-start | bytes 294920 | tf_op jit(solution)/shard_map/ppermute | solution.py:24
  7.1 1.9 %collective-permute-start.1 = (bf16[1,3,2,64,128]{4,3,2,1,0:T(8,128)(2,1)}, bf16[1,3,2,64,128]{4,3,2,1,0:T(8,128)(2,1)}, u32[]{:S(2)}, u32[]{:S(2)}) collective-permute-start(bf16[1,3,2,64,128]{4,3,2,1,0:T(8,128)(2,1)} %get-tuple-element.96), channel_id=1, source_target_pairs={{2,0},{4,2},{6,4},{8,6},{10,8},{12,10},{14,12},{16,14},{18,16},{20... | collective-permute-start | bytes 294920 | tf_op jit(solution)/shard_map/ppermute | solution.py:26
  31.8 3.6 %collective-permute-start.2 = (bf16[1,3,2,64,128]{4,3,2,1,0:T(8,128)(2,1)S(1)}, bf16[1,3,2,64,128]{4,3,2,1,0:T(8,128)(2,1)S(1)}, u32[]{:S(2)}, u32[]{:S(2)}) collective-permute-start(bf16[1,3,2,64,128]{4,3,2,1,0:T(8,128)(2,1)S(1)} %get-tuple-element.110), channel_id=1, source_target_pairs={{0,2},{2,4},{4,6},{6,8},{8,10},{10,12},{12,14},{14,16},{16,18},{18... | collective-permute-start | bytes 294920 | tf_op jit(solution)/shard_map/ppermute | solution.py:24
  37.5 3.9 %collective-permute-done.3 = bf16[1,3,2,64,128]{4,3,2,1,0:T(8,128)(2,1)S(1)} collective-permute-done((bf16[1,3,2,64,128]{4,3,2,1,0:T(8,128)(2,1)S(1)}, bf16[1,3,2,64,128]{4,3,2,1,0:T(8,128)(2,1)S(1)}, u32[]{:S(2)}, u32[]{:S(2)}) %collective-permute-start.3) | collective-permute-done | bytes 98336 | tf_op jit(solution)/shard_map/ppermute | solution.py:26
  43.0 1.9 %collective-permute-start.4 = (bf16[1,3,2,64,128]{4,3,2,1,0:T(8,128)(2,1)S(1)}, bf16[1,3,2,64,128]{4,3,2,1,0:T(8,128)(2,1)S(1)}, u32[]{:S(2)}, u32[]{:S(2)}) collective-permute-start(bf16[1,3,2,64,128]{4,3,2,1,0:T(8,128)(2,1)S(1)} %get-tuple-element.108), channel_id=1, source_target_pairs={{0,2},{2,4},{4,6},{6,8},{8,10},{10,12},{12,14},{14,16},{16,18},{18... | collective-permute-start | bytes 294920 | tf_op jit(solution)/shard_map/ppermute | solution.py:24
  44.9 2.5 %collective-permute-start.5 = (bf16[1,3,2,64,128]{4,3,2,1,0:T(8,128)(2,1)S(1)}, bf16[1,3,2,64,128]{4,3,2,1,0:T(8,128)(2,1)S(1)}, u32[]{:S(2)}, u32[]{:S(2)}) collective-permute-start(bf16[1,3,2,64,128]{4,3,2,1,0:T(8,128)(2,1)S(1)} %get-tuple-element.109), channel_id=1, source_target_pairs={{2,0},{4,2},{6,4},{8,6},{10,8},{12,10},{14,12},{16,14},{18,16},{20... | collective-permute-start | bytes 294920 | tf_op jit(solution)/shard_map/ppermute | solution.py:26
  47.5 5.1 %collective-permute-done.5 = bf16[1,3,2,64,128]{4,3,2,1,0:T(8,128)(2,1)S(1)} collective-permute-done((bf16[1,3,2,64,128]{4,3,2,1,0:T(8,128)(2,1)S(1)}, bf16[1,3,2,64,128]{4,3,2,1,0:T(8,128)(2,1)S(1)}, u32[]{:S(2)}, u32[]{:S(2)}) %collective-permute-start.5) | collective-permute-done | bytes 98336 | tf_op jit(solution)/shard_map/ppermute | solution.py:26
  54.0 1.9 %collective-permute-start.6 = (bf16[1,3,2,64,128]{4,3,2,1,0:T(8,128)(2,1)S(1)}, bf16[1,3,2,64,128]{4,3,2,1,0:T(8,128)(2,1)S(1)}, u32[]{:S(2)}, u32[]{:S(2)}) collective-permute-start(bf16[1,3,2,64,128]{4,3,2,1,0:T(8,128)(2,1)S(1)} %get-tuple-element.106), channel_id=1, source_target_pairs={{0,2},{2,4},{4,6},{6,8},{8,10},{10,12},{12,14},{14,16},{16,18},{18... | collective-permute-start | bytes 294920 | tf_op jit(solution)/shard_map/ppermute | solution.py:24
  56.0 2.4 %collective-permute-start.7 = (bf16[1,3,2,64,128]{4,3,2,1,0:T(8,128)(2,1)S(1)}, bf16[1,3,2,64,128]{4,3,2,1,0:T(8,128)(2,1)S(1)}, u32[]{:S(2)}, u32[]{:S(2)}) collective-permute-start(bf16[1,3,2,64,128]{4,3,2,1,0:T(8,128)(2,1)S(1)} %get-tuple-element.107), channel_id=1, source_target_pairs={{2,0},{4,2},{6,4},{8,6},{10,8},{12,10},{14,12},{16,14},{18,16},{20... | collective-permute-start | bytes 294920 | tf_op jit(solution)/shard_map/ppermute | solution.py:26
  58.4 4.3 %collective-permute-done.7 = bf16[1,3,2,64,128]{4,3,2,1,0:T(8,128)(2,1)S(1)} collective-permute-done((bf16[1,3,2,64,128]{4,3,2,1,0:T(8,128)(2,1)S(1)}, bf16[1,3,2,64,128]{4,3,2,1,0:T(8,128)(2,1)S(1)}, u32[]{:S(2)}, u32[]{:S(2)}) %collective-permute-start.7) | collective-permute-done | bytes 98336 | tf_op jit(solution)/shard_map/ppermute | solution.py:26
  66.3 2.4 %collective-permute-start.9 = (bf16[1,3,2,64,128]{4,3,2,1,0:T(8,128)(2,1)S(1)}, bf16[1,3,2,64,128]{4,3,2,1,0:T(8,128)(2,1)S(1)}, u32[]{:S(2)}, u32[]{:S(2)}) collective-permute-start(bf16[1,3,2,64,128]{4,3,2,1,0:T(8,128)(2,1)S(1)} %get-tuple-element.105), channel_id=1, source_target_pairs={{2,0},{4,2},{6,4},{8,6},{10,8},{12,10},{14,12},{16,14},{18,16},{20... | collective-permute-start | bytes 294920 | tf_op jit(solution)/shard_map/ppermute | solution.py:26
  68.8 4.4 %collective-permute-done.9 = bf16[1,3,2,64,128]{4,3,2,1,0:T(8,128)(2,1)S(1)} collective-permute-done((bf16[1,3,2,64,128]{4,3,2,1,0:T(8,128)(2,1)S(1)}, bf16[1,3,2,64,128]{4,3,2,1,0:T(8,128)(2,1)S(1)}, u32[]{:S(2)}, u32[]{:S(2)}) %collective-permute-start.9) | collective-permute-done | bytes 98336 | tf_op jit(solution)/shard_map/ppermute | solution.py:26
  76.5 2.6 %collective-permute-start.11 = (bf16[1,3,2,64,128]{4,3,2,1,0:T(8,128)(2,1)S(1)}, bf16[1,3,2,64,128]{4,3,2,1,0:T(8,128)(2,1)S(1)}, u32[]{:S(2)}, u32[]{:S(2)}) collective-permute-start(bf16[1,3,2,64,128]{4,3,2,1,0:T(8,128)(2,1)S(1)} %get-tuple-element.103), channel_id=1, source_target_pairs={{2,0},{4,2},{6,4},{8,6},{10,8},{12,10},{14,12},{16,14},{18,16},{20... | collective-permute-start | bytes 294920 | tf_op jit(solution)/shard_map/ppermute | solution.py:26
  79.2 4.1 %collective-permute-done.11 = bf16[1,3,2,64,128]{4,3,2,1,0:T(8,128)(2,1)S(1)} collective-permute-done((bf16[1,3,2,64,128]{4,3,2,1,0:T(8,128)(2,1)S(1)}, bf16[1,3,2,64,128]{4,3,2,1,0:T(8,128)(2,1)S(1)}, u32[]{:S(2)}, u32[]{:S(2)}) %collective-permute-start.11) | collective-permute-done | bytes 98336 | tf_op jit(solution)/shard_map/ppermute | solution.py:26
  85.2 2.6 %clamp_convert_fusion.2 = (bf16[1,9,8,64,128]{4,3,2,1,0:T(8,128)(2,1)}, bf16[1,9,8,64,128]{4,3,2,1,0:T(8,128)(2,1)}, bf16[1,9,8,64,128]{4,3,2,1,0:T(8,128)(2,1)}) fusion(f32[1,9,8,64,128]{4,3,2,1,0:T(8,128)S(1)} %get-tuple-element.20, f32[9,64,128]{2,1,0:T(8,128)S(1)} %copy-done.5, pred[9,64,128]{2,1,0:T(8,128)(4,1)S(1)} %copy-done.15, ...), kind=kLoop, calls=%fused_computation.28 | loop fusion | flops 7667712 | bytes 11206656 | tf_op jit(solution)/shard_map/convert_element_type | solution.py:128
  90.5 4.5 %fusion.11 = (f32[]{:T(128)}, f32[]{:T(128)}, f32[]{:T(128)}, f32[]{:T(128)}, f32[]{:T(128)}, /*index=5*/f32[]{:T(128)}, f32[]{:T(128)}, f32[]{:T(128)}, f32[]{:T(128)}) fusion(f32[1,9,8,64,128]{4,3,2,1,0:T(8,128)S(1)} %fusion.157, bf16[1,9,8,64,128]{4,3,2,1,0:T(8,128)(2,1)} %get-tuple-element.98, f32[9,64,128]{2,1,0:T(8,128)S(1)} %copy.35, ...), kind=kLoop, calls=%fused_computation.21 | loop fusion | flops 18284536 | bytes 11206692 | tf_op jit(solution)/shard_map/reduce_sum | solution.py:187
  95.0 1.9 %maximum_bitcast_fusion.6 = f32[1,3]{1,0:T(1,128)S(1)} fusion(f32[1]{0:T(128)} %bitcast.92, f32[1]{0:T(128)} %bitcast.91, f32[1]{0:T(128)} %bitcast.87), kind=kLoop, calls=%fused_computation.632 | loop fusion | flops 6 | bytes 24 | tf_op jit(solution)/shard_map/stack | solution.py:192
  96.9 1.9 %maximum_bitcast_fusion.7 = f32[1,3]{1,0:T(1,128)S(1)} fusion(f32[1]{0:T(128)} %bitcast.96, f32[1]{0:T(128)} %bitcast.95, f32[1]{0:T(128)} %bitcast.94), kind=kLoop, calls=%fused_computation.633 | loop fusion | flops 6 | bytes 24 | tf_op jit(solution)/shard_map/stack | solution.py:192
  98.8 2.0 %maximum_bitcast_fusion.8 = f32[1,3]{1,0:T(1,128)S(1)} fusion(f32[1]{0:T(128)} %bitcast.100, f32[1]{0:T(128)} %bitcast.99, f32[1]{0:T(128)} %bitcast.98), kind=kLoop, calls=%fused_computation.634 | loop fusion | flops 6 | bytes 24 | tf_op jit(solution)/shard_map/stack | solution.py:192
  100.9 22.3 %psum.7 = f32[3,3]{1,0:T(4,128)S(1)} all-reduce(f32[3,3]{1,0:T(4,128)S(1)} %pad_maximum_fusion.15), channel_id=1, replica_groups=mesh['space'=16,'peer'=2] {'space'}, use_global_device_ids=true, to_apply=%region_12.13 | all-reduce | flops 9 | bytes 72 | tf_op jit(solution)/shard_map/psum | solution.py:192
  124.0 17.1 %collective-permute-done.13 = bf16[1,9,8,64,128]{4,3,2,1,0:T(8,128)(2,1)} collective-permute-done((bf16[1,9,8,64,128]{4,3,2,1,0:T(8,128)(2,1)}, bf16[1,9,8,64,128]{4,3,2,1,0:T(8,128)(2,1)}, u32[]{:S(2)}, u32[]{:S(2)}) %collective-permute-start.13) | collective-permute-done | bytes 1179680 | tf_op jit(solution)/shard_map/ppermute | solution.py:40
  141.1 25.3 %collective-permute-done.14 = bf16[1,9,8,64,128]{4,3,2,1,0:T(8,128)(2,1)} collective-permute-done((bf16[1,9,8,64,128]{4,3,2,1,0:T(8,128)(2,1)}, bf16[1,9,8,64,128]{4,3,2,1,0:T(8,128)(2,1)}, u32[]{:S(2)}, u32[]{:S(2)}) %collective-permute-start.14) | collective-permute-done | bytes 1179680 | tf_op jit(solution)/shard_map/ppermute | solution.py:40
  166.4 3.4 %maximum_bitcast_fusion = bf16[1,3,9,8,64,128]{5,4,3,2,1,0:T(8,128)(2,1)} fusion(bf16[1,9,8,64,128]{4,3,2,1,0:T(8,128)(2,1)} %collective-permute-done.14, bf16[1,9,8,64,128]{4,3,2,1,0:T(8,128)(2,1)} %collective-permute-done.13, bf16[1,9,8,64,128]{4,3,2,1,0:T(8,128)(2,1)} %collective-permute-done.12), kind=kLoop, calls=%fused_computation.3 | loop fusion | flops 3538944 | bytes 7077888 | tf_op jit(solution)/shard_map/broadcast_in_dim | solution.py:194
  (154 shorter events, 40.5 us)
Async XLA Ops:
  0.6 9.2 %copy-start.2 = (f32[1,9,8,64,128]{4,3,2,1,0:T(8,128)S(1)}, f32[1,9,8,64,128]{4,3,2,1,0:T(8,128)}, u32[]{:S(2)}) copy-start(f32[1,9,8,64,128]{4,3,2,1,0:T(8,128)} %param.7) | copy-start | bytes 7077892
  2.7 8.2 %copy-start.16 = (s32[9,1,8,16]{3,2,1,0:T(8,128)S(1)}, s32[9,1,8,16]{3,2,1,0:T(8,128)}, u32[]{:S(2)}) copy-start(s32[9,1,8,16]{3,2,1,0:T(8,128)} %param.11) | copy-start | bytes 13828
  3.4 25.2 %collective-permute-start = (bf16[1,3,2,64,128]{4,3,2,1,0:T(8,128)(2,1)}, bf16[1,3,2,64,128]{4,3,2,1,0:T(8,128)(2,1)}, u32[]{:S(2)}, u32[]{:S(2)}) collective-permute-start(bf16[1,3,2,64,128]{4,3,2,1,0:T(8,128)(2,1)} %get-tuple-element.95), channel_id=1, source_target_pairs={{0,2},{2,4},{4,6},{6,8},{8,10},{10,12},{12,14},{14,16},{16,18},{18... | collective-permute-start | bytes 294920 | tf_op jit(solution)/shard_map/ppermute | solution.py:24
  7.1 21.5 %collective-permute-start.1 = (bf16[1,3,2,64,128]{4,3,2,1,0:T(8,128)(2,1)}, bf16[1,3,2,64,128]{4,3,2,1,0:T(8,128)(2,1)}, u32[]{:S(2)}, u32[]{:S(2)}) collective-permute-start(bf16[1,3,2,64,128]{4,3,2,1,0:T(8,128)(2,1)} %get-tuple-element.96), channel_id=1, source_target_pairs={{2,0},{4,2},{6,4},{8,6},{10,8},{12,10},{14,12},{16,14},{18,16},{20... | collective-permute-start | bytes 294920 | tf_op jit(solution)/shard_map/ppermute | solution.py:26
  10.8 6.0 %copy-start.17 = (f32[2,3,8]{2,0,1:T(2,128)S(1)}, f32[2,3,8]{2,0,1:T(2,128)}, u32[]{:S(2)}) copy-start(f32[2,3,8]{2,0,1:T(2,128)} %param.13) | copy-start | bytes 580
  10.8 6.0 %copy-start.18 = (s32[2,8]{1,0:T(2,128)S(1)}, s32[2,8]{1,0:T(2,128)}, u32[]{:S(2)}) copy-start(s32[2,8]{1,0:T(2,128)} %param.12) | copy-start | bytes 196
  31.8 5.7 %collective-permute-start.2 = (bf16[1,3,2,64,128]{4,3,2,1,0:T(8,128)(2,1)S(1)}, bf16[1,3,2,64,128]{4,3,2,1,0:T(8,128)(2,1)S(1)}, u32[]{:S(2)}, u32[]{:S(2)}) collective-permute-start(bf16[1,3,2,64,128]{4,3,2,1,0:T(8,128)(2,1)S(1)} %get-tuple-element.110), channel_id=1, source_target_pairs={{0,2},{2,4},{4,6},{6,8},{8,10},{10,12},{12,14},{14,16},{16,18},{18... | collective-permute-start | bytes 294920 | tf_op jit(solution)/shard_map/ppermute | solution.py:24
  35.4 5.9 %collective-permute-start.3 = (bf16[1,3,2,64,128]{4,3,2,1,0:T(8,128)(2,1)S(1)}, bf16[1,3,2,64,128]{4,3,2,1,0:T(8,128)(2,1)S(1)}, u32[]{:S(2)}, u32[]{:S(2)}) collective-permute-start(bf16[1,3,2,64,128]{4,3,2,1,0:T(8,128)(2,1)S(1)} %get-tuple-element.111), channel_id=1, source_target_pairs={{2,0},{4,2},{6,4},{8,6},{10,8},{12,10},{14,12},{16,14},{18,16},{20... | collective-permute-start | bytes 294920 | tf_op jit(solution)/shard_map/ppermute | solution.py:26
  37.4 4.2 %copy-start = (f32[8,64,128]{2,1,0:T(8,128)S(1)}, f32[8,64,128]{2,1,0:T(8,128)}, u32[]{:S(2)}) copy-start(f32[8,64,128]{2,1,0:T(8,128)} %param.10) | copy-start | bytes 786436
  37.4 4.2 %copy-start.4 = (f32[8,64,128]{2,1,0:T(8,128)S(1)}, f32[8,64,128]{2,1,0:T(8,128)}, u32[]{:S(2)}) copy-start(f32[8,64,128]{2,1,0:T(8,128)} %param.9) | copy-start | bytes 786436
  43.0 4.5 %collective-permute-start.4 = (bf16[1,3,2,64,128]{4,3,2,1,0:T(8,128)(2,1)S(1)}, bf16[1,3,2,64,128]{4,3,2,1,0:T(8,128)(2,1)S(1)}, u32[]{:S(2)}, u32[]{:S(2)}) collective-permute-start(bf16[1,3,2,64,128]{4,3,2,1,0:T(8,128)(2,1)S(1)} %get-tuple-element.108), channel_id=1, source_target_pairs={{0,2},{2,4},{4,6},{6,8},{8,10},{10,12},{12,14},{14,16},{16,18},{18... | collective-permute-start | bytes 294920 | tf_op jit(solution)/shard_map/ppermute | solution.py:24
  44.9 7.6 %collective-permute-start.5 = (bf16[1,3,2,64,128]{4,3,2,1,0:T(8,128)(2,1)S(1)}, bf16[1,3,2,64,128]{4,3,2,1,0:T(8,128)(2,1)S(1)}, u32[]{:S(2)}, u32[]{:S(2)}) collective-permute-start(bf16[1,3,2,64,128]{4,3,2,1,0:T(8,128)(2,1)S(1)} %get-tuple-element.109), channel_id=1, source_target_pairs={{2,0},{4,2},{6,4},{8,6},{10,8},{12,10},{14,12},{16,14},{18,16},{20... | collective-permute-start | bytes 294920 | tf_op jit(solution)/shard_map/ppermute | solution.py:26
  54.0 4.4 %collective-permute-start.6 = (bf16[1,3,2,64,128]{4,3,2,1,0:T(8,128)(2,1)S(1)}, bf16[1,3,2,64,128]{4,3,2,1,0:T(8,128)(2,1)S(1)}, u32[]{:S(2)}, u32[]{:S(2)}) collective-permute-start(bf16[1,3,2,64,128]{4,3,2,1,0:T(8,128)(2,1)S(1)} %get-tuple-element.106), channel_id=1, source_target_pairs={{0,2},{2,4},{4,6},{6,8},{8,10},{10,12},{12,14},{14,16},{16,18},{18... | collective-permute-start | bytes 294920 | tf_op jit(solution)/shard_map/ppermute | solution.py:24
  56.0 6.8 %collective-permute-start.7 = (bf16[1,3,2,64,128]{4,3,2,1,0:T(8,128)(2,1)S(1)}, bf16[1,3,2,64,128]{4,3,2,1,0:T(8,128)(2,1)S(1)}, u32[]{:S(2)}, u32[]{:S(2)}) collective-permute-start(bf16[1,3,2,64,128]{4,3,2,1,0:T(8,128)(2,1)S(1)} %get-tuple-element.107), channel_id=1, source_target_pairs={{2,0},{4,2},{6,4},{8,6},{10,8},{12,10},{14,12},{16,14},{18,16},{20... | collective-permute-start | bytes 294920 | tf_op jit(solution)/shard_map/ppermute | solution.py:26
  58.4 4.6 %copy-start.11 = (f32[65536]{0:T(1024)S(1)}, f32[65536]{0:T(1024)}, u32[]{:S(2)}) copy-start(f32[65536]{0:T(1024)} %scatter_custom_fusion.1) | copy-start | bytes 786436
  64.4 4.4 %collective-permute-start.8 = (bf16[1,3,2,64,128]{4,3,2,1,0:T(8,128)(2,1)S(1)}, bf16[1,3,2,64,128]{4,3,2,1,0:T(8,128)(2,1)S(1)}, u32[]{:S(2)}, u32[]{:S(2)}) collective-permute-start(bf16[1,3,2,64,128]{4,3,2,1,0:T(8,128)(2,1)S(1)} %get-tuple-element.104), channel_id=1, source_target_pairs={{0,2},{2,4},{4,6},{6,8},{8,10},{10,12},{12,14},{14,16},{16,18},{18... | collective-permute-start | bytes 294920 | tf_op jit(solution)/shard_map/ppermute | solution.py:24
  66.3 6.8 %collective-permute-start.9 = (bf16[1,3,2,64,128]{4,3,2,1,0:T(8,128)(2,1)S(1)}, bf16[1,3,2,64,128]{4,3,2,1,0:T(8,128)(2,1)S(1)}, u32[]{:S(2)}, u32[]{:S(2)}) collective-permute-start(bf16[1,3,2,64,128]{4,3,2,1,0:T(8,128)(2,1)S(1)} %get-tuple-element.105), channel_id=1, source_target_pairs={{2,0},{4,2},{6,4},{8,6},{10,8},{12,10},{14,12},{16,14},{18,16},{20... | collective-permute-start | bytes 294920 | tf_op jit(solution)/shard_map/ppermute | solution.py:26
  74.6 4.6 %collective-permute-start.10 = (bf16[1,3,2,64,128]{4,3,2,1,0:T(8,128)(2,1)S(1)}, bf16[1,3,2,64,128]{4,3,2,1,0:T(8,128)(2,1)S(1)}, u32[]{:S(2)}, u32[]{:S(2)}) collective-permute-start(bf16[1,3,2,64,128]{4,3,2,1,0:T(8,128)(2,1)S(1)} %get-tuple-element.102), channel_id=1, source_target_pairs={{0,2},{2,4},{4,6},{6,8},{8,10},{10,12},{12,14},{14,16},{16,18},{18... | collective-permute-start | bytes 294920 | tf_op jit(solution)/shard_map/ppermute | solution.py:24
  76.5 6.8 %collective-permute-start.11 = (bf16[1,3,2,64,128]{4,3,2,1,0:T(8,128)(2,1)S(1)}, bf16[1,3,2,64,128]{4,3,2,1,0:T(8,128)(2,1)S(1)}, u32[]{:S(2)}, u32[]{:S(2)}) collective-permute-start(bf16[1,3,2,64,128]{4,3,2,1,0:T(8,128)(2,1)S(1)} %get-tuple-element.103), channel_id=1, source_target_pairs={{2,0},{4,2},{6,4},{8,6},{10,8},{12,10},{14,12},{16,14},{18,16},{20... | collective-permute-start | bytes 294920 | tf_op jit(solution)/shard_map/ppermute | solution.py:26
  79.2 4.4 %copy-start.6 = (f32[65536]{0:T(1024)S(1)}, f32[65536]{0:T(1024)}, u32[]{:S(2)}) copy-start(f32[65536]{0:T(1024)} %scatter_custom_fusion.2) | copy-start | bytes 786436
  84.7 5.8 %copy-start.3 = (f32[1,9,8,64,128]{4,3,2,1,0:T(8,128)}, f32[1,9,8,64,128]{4,3,2,1,0:T(8,128)S(1)}, u32[]{:S(2)}) copy-start(f32[1,9,8,64,128]{4,3,2,1,0:T(8,128)S(1)} %fusion.157) | copy-start | bytes 7077892
  87.8 36.2 %collective-permute-start.12 = (bf16[1,9,8,64,128]{4,3,2,1,0:T(8,128)(2,1)}, bf16[1,9,8,64,128]{4,3,2,1,0:T(8,128)(2,1)}, u32[]{:S(2)}, u32[]{:S(2)}) collective-permute-start(bf16[1,9,8,64,128]{4,3,2,1,0:T(8,128)(2,1)} %get-tuple-element.97), channel_id=1, source_target_pairs={{0,1},{1,0},{2,3},{3,2},{4,5},{5,4},{6,7},{7,6},{8,9},{9,8},{10,11... | collective-permute-start | bytes 3538952 | tf_op jit(solution)/shard_map/ppermute | solution.py:40
  89.0 52.1 %collective-permute-start.13 = (bf16[1,9,8,64,128]{4,3,2,1,0:T(8,128)(2,1)}, bf16[1,9,8,64,128]{4,3,2,1,0:T(8,128)(2,1)}, u32[]{:S(2)}, u32[]{:S(2)}) collective-permute-start(bf16[1,9,8,64,128]{4,3,2,1,0:T(8,128)(2,1)} %get-tuple-element.99), channel_id=1, source_target_pairs={{0,1},{1,0},{2,3},{3,2},{4,5},{5,4},{6,7},{7,6},{8,9},{9,8},{10,11... | collective-permute-start | bytes 3538952 | tf_op jit(solution)/shard_map/ppermute | solution.py:40
  89.3 77.1 %collective-permute-start.14 = (bf16[1,9,8,64,128]{4,3,2,1,0:T(8,128)(2,1)}, bf16[1,9,8,64,128]{4,3,2,1,0:T(8,128)(2,1)}, u32[]{:S(2)}, u32[]{:S(2)}) collective-permute-start(bf16[1,9,8,64,128]{4,3,2,1,0:T(8,128)(2,1)} %get-tuple-element.98), channel_id=1, source_target_pairs={{0,1},{1,0},{2,3},{3,2},{4,5},{5,4},{6,7},{7,6},{8,9},{9,8},{10,11... | collective-permute-start | bytes 3538952 | tf_op jit(solution)/shard_map/ppermute | solution.py:40
  (10 other events, 16.6 us)
where the time goes:
time: 171 us; the launch traced here: 170 us
  waiting for transfers between devices  64.2 us (38%)
  other arithmetic  31.8 us (19%)
  starting transfers between devices  31.4 us (18%)
  blocking collectives  22.3 us (13%)
  local copies, waits for them, and re-layouts  18.6 us (11%)
    ppermute x3, waiting for transfers between devices, from_partner(): return lax.ppermute(block, axis, route)  42.4 us
    psum x1, blocking collectives, per_device(): totals = lax.psum(jnp.stack(local_sums, axis=0), 'space')  22.3 us
    ppermute x6, waiting for transfers between devices, extended(): lax.ppermute(head, axis, [((i + 1) % count, i) for i in range(ends)])  21.8 us
    ppermute x6, starting transfers between devices, extended(): lax.ppermute(tail, axis, [(i, (i + 1) % count) for i in range(ends)])  15 us
    ppermute x6, starting transfers between devices, extended(): lax.ppermute(head, axis, [((i + 1) % count, i) for i in range(ends)])  13.7 us
    eq x14, local copies, waits for them, and re-layouts, scale_tables(): chosen = expanded == exponent  8.55 us
    another operation x4, other arithmetic, per_device(): totals = lax.psum(jnp.stack(local_sums, axis=0), 'space')  5.94 us
    unnamed x21, other arithmetic  4.65 us
  transfers between devices with their start and end apart: 15, of which 7 were waited for; matrix products, arithmetic and copies ran while one was open for 18% of the time, Pallas kernels for 0%

commit v1 on v0

v1 whole, which is shorter than its diff:
```python
import functools

import jax
import jax.numpy as jnp
from jax import lax
from jax.experimental import pallas as pl
from jax.experimental.pallas import tpu as pltpu
from jax.sharding import PartitionSpec as P

BLOCK = 8
STEPS = 3
REACH = 2
W1, W2 = 9.0 / 8.0, -1.0 / 24.0
CLIP = 4.0
FLOOR = 1e-06
HALVES = 2 * STEPS
PAD = 8
ROWS = 16
LEVELS = 32700.0
TINY = 1e-30
MESH = pl.DeviceIdType.MESH

KINDS = {"stress": ((7, 8), (6,)), "velocity": ((2,), (0, 1))}
ARRIVAL = (6, 7, 8, 3, 5, 0, 4, 1, 2)


def rim_layers(kind, depth):
    back, ahead = KINDS[kind]
    up = [(c, depth - 2, -2) for c in back] + [(c, depth - 1, -1) for c in back + ahead]
    down = [(c, 0, depth) for c in back + ahead] + [(c, 1, depth + 1) for c in ahead]
    return up, down


def kernel(
    wave, buoy_in, lam_in, mu_in, exps, cells, wavelet,
    final, stored, sums,
    cur, buoy, lam, mu, up_t, down_t, tx, rx, unit_tx, unit_rx, pay, h_tx, h_rx,
    load_sem, par_sem, out_sem, pay_sem, s_send, s_recv, u_send, u_recv, h_send, h_recv,
):
    peer = lax.axis_index("peer")
    slab = lax.axis_index("space")
    count = lax.axis_size("space")
    depth, rows, cols = buoy.shape
    groups = rows // ROWS
    other = 1 - peer

    def body_of(shot, c):
        return cur.at[shot, c, pl.ds(REACH, depth), pl.ds(PAD, rows), :]

    loads = {}
    for c in ARRIVAL:
        loads[c] = pltpu.make_async_copy(wave.at[0, c], body_of(0, c), load_sem.at[c])
        loads[c].start()
    params = []
    for i, (src, dst) in enumerate(((buoy_in, buoy), (lam_in, lam), (mu_in, mu))):
        params.append(pltpu.make_async_copy(src, dst, par_sem.at[i]))
        params[-1].start()

    has_up = slab < count - 1
    has_down = slab > 0
    barrier = pltpu.get_barrier_semaphore()
    pl.semaphore_signal(barrier, inc=1, device_id={"peer": other}, device_id_type=MESH)

    @pl.when(has_up)
    def _():
        pl.semaphore_signal(barrier, inc=1, device_id={"space": slab + 1}, device_id_type=MESH)

    @pl.when(has_down)
    def _():
        pl.semaphore_signal(barrier, inc=1, device_id={"space": slab - 1}, device_id_type=MESH)

    edge_rows = jnp.zeros((PAD, cols), jnp.float32)
    edge_layer = jnp.zeros((rows, cols), jnp.float32)
    for shot in range(2):

        def clear(c, carry, shot=shot):
            for z in range(depth + 2 * REACH):
                cur[shot, c, z, pl.ds(0, PAD), :] = edge_rows
                cur[shot, c, z, pl.ds(PAD + rows, PAD), :] = edge_rows
            for z in (0, 1, depth + 2, depth + 3):
                cur[shot, c, z, pl.ds(PAD, rows), :] = edge_layer
            return carry

        lax.fori_loop(0, 9, clear, 0)

    neighbours = jnp.minimum(slab, 1) + jnp.minimum(count - 1 - slab, 1)
    pl.semaphore_wait(barrier, 1 + neighbours)

    def exchange(c):
        return pltpu.make_async_remote_copy(
            src_ref=tx.at[c], dst_ref=rx.at[c], send_sem=s_send.at[c], recv_sem=s_recv.at[c],
            device_id={"peer": other}, device_id_type=MESH,
        )

    def exchange_unit(c):
        return pltpu.make_async_remote_copy(
            src_ref=unit_tx.at[c], dst_ref=unit_rx.at[c], send_sem=u_send.at[c],
            recv_sem=u_recv.at[c], device_id={"peer": other}, device_id_type=MESH,
        )

    def halo(h, way, size):
        target = slab + 1 if way == 0 else slab - 1
        return pltpu.make_async_remote_copy(
            src_ref=h_tx.at[h, way, pl.ds(0, size)], dst_ref=h_rx.at[h, way, pl.ds(0, size)],
            send_sem=h_send.at[h, way], recv_sem=h_recv.at[h, way],
            device_id={"space": target}, device_id_type=MESH,
        )

    def send_rims(shot, kind, h):
        for way, layers in enumerate(rim_layers(kind, depth)):
            for i, (c, z, _) in enumerate(layers):
                h_tx[h, way, i] = cur[shot, c, REACH + z, pl.ds(PAD, rows), :].astype(jnp.bfloat16)

            @pl.when(has_up if way == 0 else has_down)
            def _():
                halo(h, way, len(layers)).start()

    def take_rims(shot, kind, h):
        for way, layers in enumerate(rim_layers(kind, depth)):

            @pl.when(has_down if way == 0 else has_up)
            def _():
                halo(h, way, len(layers)).wait_recv()
                for i, (c, _, z) in enumerate(layers):
                    cur[shot, c, REACH + z, pl.ds(PAD, rows), :] = h_rx[h, way, i].astype(
                        jnp.float32
                    )

    def finish_sends(kind, h):
        for way, layers in enumerate(rim_layers(kind, depth)):

            @pl.when(has_up if way == 0 else has_down)
            def _():
                halo(h, way, len(layers)).wait_send()

    lane = lax.broadcasted_iota(jnp.int32, (ROWS, cols), 1)
    row = lax.broadcasted_iota(jnp.int32, (ROWS, cols), 0)
    spot = row * cols + lane

    def shifted(f, k):
        moved = pltpu.roll(f, (-k) % cols, 1)
        keep = lane < cols - k if k > 0 else lane >= -k
        return jnp.where(keep, moved, 0.0)

    def along_x(f, ahead):
        if ahead:
            return W1 * (shifted(f, 1) - f) + W2 * (shifted(f, 2) - shifted(f, -1))
        return W1 * (f - shifted(f, -1)) + W2 * (shifted(f, 1) - shifted(f, -2))

    def reader(shot, z, g):
        base = PAD + g * ROWS

        def read(c, dz=0, dy=0):
            return cur[shot, c, z + (REACH + dz), pl.ds(base + dy, ROWS), :]

        def along_y(c, ahead):
            o = 1 if ahead else 0
            return W1 * (read(c, 0, o) - read(c, 0, o - 1)) + W2 * (
                read(c, 0, o + 1) - read(c, 0, o - 2)
            )

        def along_z(c, ahead):
            o = 1 if ahead else 0
            return W1 * (read(c, o) - read(c, o - 1)) + W2 * (read(c, o + 1) - read(c, o - 2))

        def write(c, value):
            cur[shot, c, z + REACH, pl.ds(base, ROWS), :] = value

        return read, along_y, along_z, write

    def velocity_layer(shot, z):
        for g in range(groups):
            read, along_y, along_z, write = reader(shot, z, g)
            b = buoy[z, pl.ds(g * ROWS, ROWS), :]
            write(0, read(0) + b * (along_x(read(3), True) + along_y(5, False) + along_z(7, False)))
            write(1, read(1) + b * (along_x(read(5), False) + along_y(4, True) + along_z(8, False)))
            write(2, read(2) + b * (along_x(read(7), False) + along_y(8, False) + along_z(6, True)))

    def stress_layer(shot, t, z, totals):
        shot_index = peer if shot == 0 else other
        for g in range(groups):
            read, along_y, along_z, write = reader(shot, z, g)
            part = pl.ds(g * ROWS, ROWS)
            vx, vy, vz = read(0), read(1), read(2)
            ex, ey, ez = along_x(vx, False), along_y(1, False), along_z(2, False)
            image = jnp.zeros((ROWS, cols), jnp.float32)
            start = ((slab * depth + z) * rows + g * ROWS) * cols
            for j in range(cells.shape[1]):
                image = image + jnp.where(
                    spot == cells[shot_index, j] - start, wavelet[shot_index, t, j], 0.0
                )
            m = mu[z, part, :]
            pressure = lam[z, part, :] * (ex + ey + ez) + image
            twice = 2.0 * m
            values = [
                vx, vy, vz,
                read(3) + pressure + twice * ex,
                read(4) + pressure + twice * ey,
                read(5) + m * (along_y(0, True) + along_x(vy, True)),
                read(6) + pressure + twice * ez,
                read(7) + m * (along_z(0, True) + along_x(vz, True)),
                read(8) + m * (along_z(1, True) + along_y(2, True)),
            ]
            for c in range(3, 9):
                write(c, values[c])
            for c in range(9):
                v = values[c]
                packed = jnp.clip(v * down_t[c, part, :], -CLIP, CLIP).astype(jnp.bfloat16)
                if shot == 1:
                    pay[t, c, z, part, :] = packed
                else:
                    level = packed.astype(jnp.float32)
                    miss = v - level * up_t[c, part, :]
                    totals = (
                        totals[0] + jnp.abs(level),
                        totals[1] + miss * miss,
                        totals[2] + v * v,
                    )
        return totals

    nothing = jnp.zeros((ROWS, cols), jnp.float32)

    def inner(k):
        return k + 2

    def outer(k):
        return jnp.where(k < 2, k, k + (depth - 4))

    def half(shot, i):
        t, h = i // 2, shot * HALVES + i
        kind = "stress" if i % 2 == 0 else "velocity"
        if i % 2 == 0:

            def run(place, size, totals):
                def step(k, carry):
                    velocity_layer(shot, place(k))
                    return carry

                lax.fori_loop(0, size, step, 0)
                return totals
        else:

            def run(place, size, totals):
                def step(k, carry):
                    return stress_layer(shot, t, place(k), carry)

                return lax.fori_loop(0, size, step, totals)

        totals = run(inner, depth - 4, (nothing,) * 3)
        take_rims(shot, kind, h)
        totals = run(outer, 4, totals)
        if i < HALVES - 1:
            send_rims(shot, "velocity" if i % 2 == 0 else "stress", h + 1)
        if i % 2 and shot == 0:
            for s in range(3):
                sums[t, s] = totals[s]
        if i % 2 and shot == 1:
            payload_out(t).start()

    def payload_out(t):
        return pltpu.make_async_copy(pay.at[t], stored.at[0, t], pay_sem.at[t])

    def field_out(c):
        return pltpu.make_async_copy(body_of(0, c), final.at[0, c], out_sem.at[c])

    def unpack(c):
        exchange_unit(c).wait_recv()
        exchange(c).wait_recv()
        unit = unit_rx[c]

        def step(z, carry):
            for g in range(groups):
                whole = rx[c, z, pl.ds(g * ROWS, ROWS), :].astype(jnp.int32)
                cur[1, c, z + REACH, pl.ds(PAD + g * ROWS, ROWS), :] = (
                    whole.astype(jnp.float32) * unit
                )
            return carry

        lax.fori_loop(0, depth, step, 0)

    for c in ARRIVAL:
        loads[c].wait()

        def largest(z, top, c=c):
            for g in range(groups):
                top = jnp.maximum(
                    top, jnp.abs(cur[0, c, z + REACH, pl.ds(PAD + g * ROWS, ROWS), :])
                )
            return top

        top = lax.fori_loop(0, depth, largest, jnp.full((ROWS, cols), TINY, jnp.float32))
        unit_tx[c] = top * (1.0 / LEVELS)
        inverse = LEVELS / top

        def pack(z, carry, c=c, inverse=inverse):
            for g in range(groups):
                value = cur[0, c, z + REACH, pl.ds(PAD + g * ROWS, ROWS), :] * inverse
                tx[c, z, pl.ds(g * ROWS, ROWS), :] = (
                    jnp.round(value).astype(jnp.int32).astype(jnp.int16)
                )
            return carry

        lax.fori_loop(0, depth, pack, 0)
        exchange_unit(c).start()
        exchange(c).start()
        if c == 8:
            send_rims(0, "stress", 0)

    bands, strips = exps.shape[1], exps.shape[2]
    spread_y = (
        lax.broadcasted_iota(jnp.int32, (rows, bands), 0) // BLOCK
        == lax.broadcasted_iota(jnp.int32, (rows, bands), 1)
    ).astype(jnp.float32)
    spread_x = (
        lax.broadcasted_iota(jnp.int32, (strips, cols), 1) // BLOCK
        == lax.broadcasted_iota(jnp.int32, (strips, cols), 0)
    ).astype(jnp.float32)
    for c in range(9):
        e = exps[c]
        for table, sign in ((up_t, 1), (down_t, -1)):
            scale = jnp.zeros(e.shape, jnp.float32)
            for power in range(-2, 3):
                scale = jnp.where(e == power, jnp.float32(2.0 ** (sign * power)), scale)
            wide = jnp.dot(scale, spread_x, preferred_element_type=jnp.float32)
            table[c] = jnp.dot(spread_y, wide, preferred_element_type=jnp.float32)

    for p in params:
        p.wait()
    half(0, 0)
    half(0, 1)
    half(0, 2)
    for c in ARRIVAL[:3]:
        unpack(c)
    send_rims(1, "stress", HALVES)
    half(0, 3)
    for c in ARRIVAL[3:]:
        unpack(c)
    half(1, 0)
    half(0, 4)
    half(1, 1)
    half(0, 5)
    for c in range(9):
        field_out(c).start()
    for i in range(2, HALVES):
        half(1, i)

    for c in ARRIVAL:
        exchange(c).wait_send()
        exchange_unit(c).wait_send()
    for shot in range(2):
        for i in range(HALVES):
            finish_sends("stress" if i % 2 == 0 else "velocity", shot * HALVES + i)
    for c in range(9):
        field_out(c).wait()
    for t in range(STEPS):
        payload_out(t).wait()


def per_device(wavefield, buoyancy, lame_lambda, shear_modulus, exponents, cells, wavelet):
    _, parts, depth, rows, cols = wavefield.shape
    cell_count = parts * depth * rows * cols * lax.axis_size("space")
    f32, bf16 = jnp.float32, jnp.bfloat16
    anywhere = pl.BlockSpec(memory_space=pl.ANY)
    vmem = pl.BlockSpec(memory_space=pltpu.VMEM)
    smem = pl.BlockSpec(memory_space=pltpu.SMEM)
    dma = pltpu.SemaphoreType.DMA
    final, stored, sums = pl.pallas_call(
        kernel,
        out_shape=(
            jax.ShapeDtypeStruct(wavefield.shape, f32),
            jax.ShapeDtypeStruct((1, STEPS, parts, depth, rows, cols), bf16),
            jax.ShapeDtypeStruct((STEPS, 3, ROWS, cols), f32),
        ),
        in_specs=[anywhere] * 4 + [vmem, smem, smem],
        out_specs=(anywhere, anywhere, vmem),
        scratch_shapes=[
            pltpu.VMEM((2, parts, depth + 2 * REACH, rows + 2 * PAD, cols), f32),
            pltpu.VMEM((depth, rows, cols), f32),
            pltpu.VMEM((depth, rows, cols), f32),
            pltpu.VMEM((depth, rows, cols), f32),
            pltpu.VMEM((parts, rows, cols), f32),
            pltpu.VMEM((parts, rows, cols), f32),
            pltpu.VMEM((parts, depth, rows, cols), jnp.int16),
            pltpu.VMEM((parts, depth, rows, cols), jnp.int16),
            pltpu.VMEM((parts, ROWS, cols), f32),
            pltpu.VMEM((parts, ROWS, cols), f32),
            pltpu.VMEM((STEPS, parts, depth, rows, cols), bf16),
            pltpu.VMEM((2 * HALVES, 2, 5, rows, cols), bf16),
            pltpu.VMEM((2 * HALVES, 2, 5, rows, cols), bf16),
            dma((parts,)), dma((3,)), dma((parts,)), dma((STEPS,)),
            dma((parts,)), dma((parts,)), dma((parts,)), dma((parts,)),
            dma((2 * HALVES, 2)), dma((2 * HALVES, 2)),
        ],
        compiler_params=pltpu.CompilerParams(
            collective_id=0, has_side_effects=True, vmem_limit_bytes=48 * 1024 * 1024
        ),
        name="two_shots",
    )(wavefield, buoyancy, lame_lambda, shear_modulus, exponents[:, 0], cells, wavelet)
    totals = lax.psum(jnp.sum(sums, axis=(2, 3)), "space")
    mean_size = totals[:, 0] / cell_count
    relative = totals[:, 1] / cell_count / (totals[:, 2] / cell_count + FLOOR)
    statistics = jnp.stack([mean_size, jnp.sqrt(relative)], axis=-1)[None]
    return final, stored, statistics


def solution(mesh):
    return jax.shard_map(
        per_device,
        mesh=mesh,
        in_specs=(
            P("peer", None, "space", None, None),
            P("space", None, None),
            P("space", None, None),
            P("space", None, None),
            P(None, "space", None, None),
            P(),
            P(),
        ),
        out_specs=(
            P("peer", None, "space", None, None),
            P("peer", None, None, "space", None, None),
            P("peer", None, None),
        ),
        check_vma=False,
    )
```

time: 171 us -> 100 us (0.58)
  the two profiles are of different devices: /device:TPU:9 before, /device:TPU:0 now
where the time goes in v1:
time: 100 us
  Pallas kernels  52 us (52%)
  blocking collectives  35.1 us (35%)
  local copies, waits for them, and re-layouts  12 us (12%)
    pallas_call x1, Pallas kernels, per_device(): pl.pallas_call(kernel, out_shape=(jax.ShapeDtypeStruct(wavefield.shape, f...  52 us
    psum x1, blocking collectives, per_device(): totals = lax.psum(jnp.sum(sums, axis=(2, 3)), 'space')  35.1 us
    unnamed x17, local copies, waits for them, and re-layouts  11.3 us

profile of v1, /device:TPU:0, one launch (start us, length us, event | category | flops | bytes accessed | tf_op | source)
XLA Modules:
  0.0 100.0 jit_solution(1514666759457560060)
XLA Ops:
  0.6 0.7 copy.11.wavelet
  1.3 0.0 copy-start
  1.3 1.7 %copy-done = f32[1,9,8,64,128]{4,3,2,1,0:T(8,128)S(1)} copy-done((f32[1,9,8,64,128]{4,3,2,1,0:T(8,128)S(1)}, f32[1,9,8,64,128]{4,3,2,1,0:T(8,128)}, u32[]{:S(2)}) %copy-start) | copy-done | bytes 2359320
  3.0 0.0 copy-start.1
  3.0 0.9 copy-done.1
  3.9 0.0 copy-start.2
  3.9 0.9 copy-done.2
  4.9 0.0 copy-start.3
  4.9 0.9 copy-done.3
  5.8 0.0 copy-start.4
  5.8 0.8 copy-done.4
  6.6 0.0 copy-start.5
  6.6 0.7 copy-done.5
  7.3 52.0 %two_shots.1 = (f32[1,9,8,64,128]{4,3,2,1,0:T(8,128)S(1)}, bf16[1,3,9,8,64,128]{5,4,3,2,1,0:T(8,128)(2,1)}, f32[3,3,16,128]{3,2,1,0:T(8,128)S(1)}) custom-call(f32[1,9,8,64,128]{4,3,2,1,0:T(8,128)S(1)} %copy-done, f32[8,64,128]{2,1,0:T(8,128)S(1)} %copy-done.1, f32[8,64,128]{2,1,0:T(8,128)S(1)} %copy-done.2, f32[8,64,128]{2,1,0:T(8,128)S(1)} %copy-done.3, ...), custom_call_target="tpu_custom_call" | custom-call | tf_op jit(solution)/shard_map/two_shots/pallas_call | solution.py:367
  59.3 0.1 reduce_sum.9
  59.4 35.1 %psum.7 = f32[3,3]{1,0:T(4,128)S(1)} all-reduce(f32[3,3]{1,0:T(4,128)S(1)} %reduce_sum.9), channel_id=1, replica_groups=mesh['space'=16,'peer'=2] {'space'}, use_global_device_ids=true, to_apply=%region_1.0 | all-reduce | flops 9 | bytes 72 | tf_op jit(solution)/shard_map/psum | solution.py:399
  94.5 0.1 slice_multiply_fusion
  94.6 0.1 pad_maximum_fusion
  94.7 0.7 copy.12
  95.4 0.0 copy-start.6
  95.4 1.4 %copy.15 = f32[1,9,8,64,128]{4,3,2,1,0:T(8,128)} copy(f32[1,9,8,64,128]{4,3,2,1,0:T(8,128)S(1)} %get-tuple-element.14) | data formatting | bytes 4718592
  96.8 1.4 %copy-done.6 = bf16[1,3,9,8,64,128]{5,4,3,2,1,0:T(8,128)(2,1)S(1)} copy-done((bf16[1,3,9,8,64,128]{5,4,3,2,1,0:T(8,128)(2,1)S(1)}, bf16[1,3,9,8,64,128]{5,4,3,2,1,0:T(8,128)(2,1)}, u32[]{:S(2)}) %copy-start.6) | copy-done | bytes 3538968
  98.2 1.8 %copy.16 = bf16[1,3,9,8,64,128]{5,4,3,2,1,0:T(8,128)(2,1)} copy(bf16[1,3,9,8,64,128]{5,4,3,2,1,0:T(8,128)(2,1)S(1)} %copy-done.6) | data formatting | bytes 7077888
Async XLA Ops:
  1.3 1.7 %copy-start = (f32[1,9,8,64,128]{4,3,2,1,0:T(8,128)S(1)}, f32[1,9,8,64,128]{4,3,2,1,0:T(8,128)}, u32[]{:S(2)}) copy-start(f32[1,9,8,64,128]{4,3,2,1,0:T(8,128)} %wave.1) | copy-start | bytes 7077892
  3.0 0.9 copy-start.1
  3.9 0.9 copy-start.2
  4.9 0.9 copy-start.3
  5.8 0.8 copy-start.4
  6.6 0.7 copy-start.5
  95.4 2.9 %copy-start.6 = (bf16[1,3,9,8,64,128]{5,4,3,2,1,0:T(8,128)(2,1)S(1)}, bf16[1,3,9,8,64,128]{5,4,3,2,1,0:T(8,128)(2,1)}, u32[]{:S(2)}) copy-start(bf16[1,3,9,8,64,128]{5,4,3,2,1,0:T(8,128)(2,1)} %get-tuple-element.15) | copy-start | bytes 10616836

commit v2 on v1

--- a/solution.py
+++ b/solution.py
@@ -31,11 +31,15 @@
     return up, down
 
 
+def partner_of(slab, r):
+    return slab + (1 << r) * (1 - 2 * ((slab // (1 << r)) % 2))
+
+
 def kernel(
-    wave, buoy_in, lam_in, mu_in, exps, cells, wavelet,
-    final, stored, sums,
-    cur, buoy, lam, mu, up_t, down_t, tx, rx, unit_tx, unit_rx, pay, h_tx, h_rx,
-    load_sem, par_sem, out_sem, pay_sem, s_send, s_recv, u_send, u_recv, h_send, h_recv,
+    wave, buoy_in, lam_in, mu_in, exps_in, cells, wavelet,
+    final, stored, statistics,
+    cur, buoy, lam, mu, up_t, down_t, tx, rx, unit_tx, unit_rx, pay, h_tx, h_rx, exps, sum_tx, sum_rx,
+    load_sem, par_sem, out_sem, pay_sem, s_send, s_recv, u_send, u_recv, h_send, h_recv, r_send, r_recv,
 ):
     peer = lax.axis_index("peer")
     slab = lax.axis_index("space")
@@ -43,6 +47,7 @@
     depth, rows, cols = buoy.shape
     groups = rows // ROWS
     other = 1 - peer
+    rounds = count.bit_length() - 1
 
     def body_of(shot, c):
         return cur.at[shot, c, pl.ds(REACH, depth), pl.ds(PAD, rows), :]
@@ -52,7 +57,7 @@
         loads[c] = pltpu.make_async_copy(wave.at[0, c], body_of(0, c), load_sem.at[c])
         loads[c].start()
     params = []
-    for i, (src, dst) in enumerate(((buoy_in, buoy), (lam_in, lam), (mu_in, mu))):
+    for i, (src, dst) in enumerate(((buoy_in, buoy), (lam_in, lam), (mu_in, mu), (exps_in.at[:, 0], exps))):
         params.append(pltpu.make_async_copy(src, dst, par_sem.at[i]))
         params[-1].start()
 
@@ -69,8 +74,14 @@
     def _():
         pl.semaphore_signal(barrier, inc=1, device_id={"space": slab - 1}, device_id_type=MESH)
 
+    for r in range(1, rounds):
+        pl.semaphore_signal(
+            barrier, inc=1, device_id={"space": partner_of(slab, r)}, device_id_type=MESH
+        )
+
     edge_rows = jnp.zeros((PAD, cols), jnp.float32)
     edge_layer = jnp.zeros((rows, cols), jnp.float32)
+    sum_tx[0] = jnp.zeros((ROWS, cols), jnp.float32)
     for shot in range(2):
 
         def clear(c, carry, shot=shot):
@@ -84,7 +95,7 @@
         lax.fori_loop(0, 9, clear, 0)
 
     neighbours = jnp.minimum(slab, 1) + jnp.minimum(count - 1 - slab, 1)
-    pl.semaphore_wait(barrier, 1 + neighbours)
+    pl.semaphore_wait(barrier, rounds + neighbours)
 
     def exchange(c):
         return pltpu.make_async_remote_copy(
@@ -187,7 +198,7 @@
             start = ((slab * depth + z) * rows + g * ROWS) * cols
             for j in range(cells.shape[1]):
                 image = image + jnp.where(
-                    spot == cells[shot_index, j] - start, wavelet[shot_index, t, j], 0.0
+                    spot == cells[shot_index, j] - start, wavelet[t, shot_index, j], 0.0
                 )
             m = mu[z, part, :]
             pressure = lam[z, part, :] * (ex + ey + ez) + image
@@ -253,7 +264,8 @@
             send_rims(shot, "velocity" if i % 2 == 0 else "stress", h + 1)
         if i % 2 and shot == 0:
             for s in range(3):
-                sums[t, s] = totals[s]
+                line = jnp.sum(totals[s], axis=0, keepdims=True)
+                sum_tx[0, pl.ds(3 * t + s, 1), :] = line
         if i % 2 and shot == 1:
             payload_out(t).start()
 
@@ -262,6 +274,32 @@
 
     def field_out(c):
         return pltpu.make_async_copy(body_of(0, c), final.at[0, c], out_sem.at[c])
+
+    def swap_sums(r):
+        return pltpu.make_async_remote_copy(
+            src_ref=sum_tx.at[r], dst_ref=sum_rx.at[r], send_sem=r_send.at[r],
+            recv_sem=r_recv.at[r], device_id={"space": partner_of(slab, r)}, device_id_type=MESH,
+        )
+
+    def add_sums(r):
+        swap_sums(r).wait_recv()
+        sum_tx[r + 1] = sum_tx[r] + sum_rx[r]
+        if r + 1 < rounds:
+            swap_sums(r + 1).start()
+
+    def write_statistics():
+        total = jnp.sum(sum_tx[rounds], axis=1, keepdims=True)
+        cells_in_all = jnp.float32(9 * depth * rows * cols * count)
+        at_row = lax.broadcasted_iota(jnp.int32, (STEPS, 2), 0)
+        at_column = lax.broadcasted_iota(jnp.int32, (STEPS, 2), 1)
+        result = jnp.zeros((STEPS, 2), jnp.float32)
+        for t in range(STEPS):
+            size, miss, power = (total[3 * t + s : 3 * t + s + 1] / cells_in_all for s in range(3))
+            relative = jnp.sqrt(miss / (power + FLOOR))
+            result = jnp.where(
+                at_row == t, jnp.where(at_column == 0, size, relative), result
+            )
+        statistics[0] = result
 
     def unpack(c):
         exchange_unit(c).wait_recv()
@@ -315,6 +353,7 @@
         lax.broadcasted_iota(jnp.int32, (strips, cols), 1) // BLOCK
         == lax.broadcasted_iota(jnp.int32, (strips, cols), 0)
     ).astype(jnp.float32)
+    params.pop().wait()
     for c in range(9):
         e = exps[c]
         for table, sign in ((up_t, 1), (down_t, -1)):
@@ -339,10 +378,20 @@
     half(0, 4)
     half(1, 1)
     half(0, 5)
+    swap_sums(0).start()
     for c in range(9):
         field_out(c).start()
+    done = 0
     for i in range(2, HALVES):
         half(1, i)
+        if done < rounds:
+            add_sums(done)
+            done += 1
+    for r in range(done, rounds):
+        add_sums(r)
+    write_statistics()
+    for r in range(rounds):
+        swap_sums(r).wait_send()
 
     for c in ARRIVAL:
         exchange(c).wait_send()
@@ -358,20 +407,20 @@
 
 def per_device(wavefield, buoyancy, lame_lambda, shear_modulus, exponents, cells, wavelet):
     _, parts, depth, rows, cols = wavefield.shape
-    cell_count = parts * depth * rows * cols * lax.axis_size("space")
+    rounds = lax.axis_size("space").bit_length() - 1
     f32, bf16 = jnp.float32, jnp.bfloat16
     anywhere = pl.BlockSpec(memory_space=pl.ANY)
     vmem = pl.BlockSpec(memory_space=pltpu.VMEM)
     smem = pl.BlockSpec(memory_space=pltpu.SMEM)
     dma = pltpu.SemaphoreType.DMA
-    final, stored, sums = pl.pallas_call(
+    return pl.pallas_call(
         kernel,
         out_shape=(
             jax.ShapeDtypeStruct(wavefield.shape, f32),
             jax.ShapeDtypeStruct((1, STEPS, parts, depth, rows, cols), bf16),
-            jax.ShapeDtypeStruct((STEPS, 3, ROWS, cols), f32),
+            jax.ShapeDtypeStruct((1, STEPS, 2), f32),
         ),
-        in_specs=[anywhere] * 4 + [vmem, smem, smem],
+        in_specs=[anywhere] * 5 + [smem, smem],
         out_specs=(anywhere, anywhere, vmem),
         scratch_shapes=[
             pltpu.VMEM((2, parts, depth + 2 * REACH, rows + 2 * PAD, cols), f32),
@@ -387,20 +436,18 @@
             pltpu.VMEM((STEPS, parts, depth, rows, cols), bf16),
             pltpu.VMEM((2 * HALVES, 2, 5, rows, cols), bf16),
             pltpu.VMEM((2 * HALVES, 2, 5, rows, cols), bf16),
-            dma((parts,)), dma((3,)), dma((parts,)), dma((STEPS,)),
+            pltpu.VMEM((parts,) + exponents.shape[2:], jnp.int32),
+            pltpu.VMEM((rounds + 1, ROWS, cols), f32),
+            pltpu.VMEM((rounds, ROWS, cols), f32),
+            dma((parts,)), dma((4,)), dma((parts,)), dma((STEPS,)),
             dma((parts,)), dma((parts,)), dma((parts,)), dma((parts,)),
-            dma((2 * HALVES, 2)), dma((2 * HALVES, 2)),
+            dma((2 * HALVES, 2)), dma((2 * HALVES, 2)), dma((rounds,)), dma((rounds,)),
         ],
         compiler_params=pltpu.CompilerParams(
-            collective_id=0, has_side_effects=True, vmem_limit_bytes=48 * 1024 * 1024
+            collective_id=0, has_side_effects=True, vmem_limit_bytes=67043328
         ),
         name="two_shots",
-    )(wavefield, buoyancy, lame_lambda, shear_modulus, exponents[:, 0], cells, wavelet)
-    totals = lax.psum(jnp.sum(sums, axis=(2, 3)), "space")
-    mean_size = totals[:, 0] / cell_count
-    relative = totals[:, 1] / cell_count / (totals[:, 2] / cell_count + FLOOR)
-    statistics = jnp.stack([mean_size, jnp.sqrt(relative)], axis=-1)[None]
-    return final, stored, statistics
+    )(wavefield, buoyancy, lame_lambda, shear_modulus, exponents, cells, wavelet.transpose(1, 0, 2))
 
 
 def solution(mesh):

time: 100 us -> 65.4 us (0.65)
  blocking collectives: 35.1 us -> 0 us
  Pallas kernels: 52 us -> 58 us
  local copies, waits for them, and re-layouts: 12 us -> 6.6 us
    psum x1 -> x0, blocking collectives: 35.1 us -> none  [per_device(): totals = lax.psum(jnp.sum(sums, axis=(2, 3)), 'space')]
    unnamed x17 -> x4, local copies, waits for them, and re-layouts: 11.3 us -> 5.31 us
    pallas_call x1, Pallas kernels: 52 us -> 58 us  [per_device(): pl.pallas_call(kernel, out_shape=(jax.ShapeDtypeStruct(wavefield.shape, f...]
    pallas_call x0 -> x1, local copies, waits for them, and re-layouts: none -> 1.3 us  [per_device(): pl.pallas_call(kernel, out_shape=(jax.ShapeDtypeStruct(wavefield.shape, f...]
where the time goes in v2:
time: 65.4 us; the launch traced here: 65.2 us
  Pallas kernels  58 us (89%)
  local copies, waits for them, and re-layouts  6.6 us (10%)
    pallas_call x1, Pallas kernels, per_device(): pl.pallas_call(kernel, out_shape=(jax.ShapeDtypeStruct(wavefield.shape, f...  58 us
    unnamed x4, local copies, waits for them, and re-layouts  5.31 us

profile of v2, /device:TPU:0, one launch (start us, length us, event | category | flops | bytes accessed | tf_op | source)
XLA Modules:
  0.0 65.2 jit_solution(18230585141209042937)
XLA Ops:
  0.6 58.0 %two_shots.1 = (f32[1,9,8,64,128]{4,3,2,1,0:T(8,128)}, bf16[1,3,9,8,64,128]{5,4,3,2,1,0:T(8,128)(2,1)}, f32[1,3,2]{2,1,0:T(4,128)}) custom-call(f32[1,9,8,64,128]{4,3,2,1,0:T(8,128)} %wave.1, f32[8,64,128]{2,1,0:T(8,128)} %buoy_in.1, f32[8,64,128]{2,1,0:T(8,128)} %lam_in.1, f32[8,64,128]{2,1,0:T(8,128)} %mu_in.1, s32[9,1,8,16]{3,2,1,0:T(8,128)} %exps_in.1, ...), custom_call_target="tpu_custom_call" | custom-call | tf_op jit(solution)/shard_map/two_shots/pallas_call | solution.py:416
  58.6 1.3 %copy.10 = f32[1,3,2]{1,2,0:T(2,128)} copy(f32[1,3,2]{2,1,0:T(4,128)} %get-tuple-element.5) | data formatting | bytes 48 | tf_op jit(solution)/shard_map/two_shots/pallas_call | solution.py:416
  59.9 0.0 copy-start
  59.9 3.5 %copy.13 = f32[1,9,8,64,128]{4,3,2,1,0:T(8,128)} copy(f32[1,9,8,64,128]{4,3,2,1,0:T(8,128)} %get-tuple-element.9) | data formatting | bytes 4718592
  63.4 0.0 copy-done
  63.4 1.8 %copy.14 = bf16[1,3,9,8,64,128]{5,4,3,2,1,0:T(8,128)(2,1)} copy(bf16[1,3,9,8,64,128]{5,4,3,2,1,0:T(8,128)(2,1)S(1)} %copy-done) | data formatting | bytes 7077888
Async XLA Ops:
  59.9 3.5 %copy-start = (bf16[1,3,9,8,64,128]{5,4,3,2,1,0:T(8,128)(2,1)S(1)}, bf16[1,3,9,8,64,128]{5,4,3,2,1,0:T(8,128)(2,1)}, u32[]{:S(2)}) copy-start(bf16[1,3,9,8,64,128]{5,4,3,2,1,0:T(8,128)(2,1)} %get-tuple-element.10) | copy-start | bytes 10616836

commit v3 on v2

--- a/solution.py
+++ b/solution.py
@@ -16,6 +16,7 @@
 HALVES = 2 * STEPS
 PAD = 8
 ROWS = 16
+HANDED = 2
 LEVELS = 32700.0
 TINY = 1e-30
 MESH = pl.DeviceIdType.MESH
@@ -39,7 +40,7 @@
     wave, buoy_in, lam_in, mu_in, exps_in, cells, wavelet,
     final, stored, statistics,
     cur, buoy, lam, mu, up_t, down_t, tx, rx, unit_tx, unit_rx, pay, h_tx, h_rx, exps, sum_tx, sum_rx,
-    load_sem, par_sem, out_sem, pay_sem, s_send, s_recv, u_send, u_recv, h_send, h_recv, r_send, r_recv,
+    load_sem, par_sem, out_sem, pay_sem, s_send, s_recv, u_send, u_recv, h_send, h_recv, f_send, f_recv, r_send, r_recv,
 ):
     peer = lax.axis_index("peer")
     slab = lax.axis_index("space")
@@ -117,6 +118,14 @@
             device_id={"space": target}, device_id_type=MESH,
         )
 
+    def handed(i, way, size):
+        return pltpu.make_async_remote_copy(
+            src_ref=h_rx.at[i, way, pl.ds(0, size)],
+            dst_ref=h_rx.at[HALVES + i, way, pl.ds(0, size)],
+            send_sem=f_send.at[i, way], recv_sem=f_recv.at[i, way],
+            device_id={"peer": other}, device_id_type=MESH,
+        )
+
     def send_rims(shot, kind, h):
         for way, layers in enumerate(rim_layers(kind, depth)):
             for i, (c, z, _) in enumerate(layers):
@@ -131,7 +140,12 @@
 
             @pl.when(has_down if way == 0 else has_up)
             def _():
-                halo(h, way, len(layers)).wait_recv()
+                if shot == 1 and h - HALVES >= HANDED:
+                    handed(h - HALVES, way, len(layers)).wait_recv()
+                else:
+                    halo(h, way, len(layers)).wait_recv()
+                if shot == 0 and h >= HANDED:
+                    handed(h, way, len(layers)).start()
                 for i, (c, _, z) in enumerate(layers):
                     cur[shot, c, REACH + z, pl.ds(PAD, rows), :] = h_rx[h, way, i].astype(
                         jnp.float32
@@ -143,6 +157,13 @@
             @pl.when(has_up if way == 0 else has_down)
             def _():
                 halo(h, way, len(layers)).wait_send()
+
+    def finish_handed(kind, i):
+        for way, layers in enumerate(rim_layers(kind, depth)):
+
+            @pl.when(has_down if way == 0 else has_up)
+            def _():
+                handed(i, way, len(layers)).wait_send()
 
     lane = lax.broadcasted_iota(jnp.int32, (ROWS, cols), 1)
     row = lax.broadcasted_iota(jnp.int32, (ROWS, cols), 0)
@@ -260,7 +281,7 @@
         totals = run(inner, depth - 4, (nothing,) * 3)
         take_rims(shot, kind, h)
         totals = run(outer, 4, totals)
-        if i < HALVES - 1:
+        if i < HALVES - 1 and (shot == 0 or i + 1 < HANDED):
             send_rims(shot, "velocity" if i % 2 == 0 else "stress", h + 1)
         if i % 2 and shot == 0:
             for s in range(3):
@@ -398,7 +419,11 @@
         exchange_unit(c).wait_send()
     for shot in range(2):
         for i in range(HALVES):
-            finish_sends("stress" if i % 2 == 0 else "velocity", shot * HALVES + i)
+            kind = "stress" if i % 2 == 0 else "velocity"
+            if shot == 0 or i < HANDED:
+                finish_sends(kind, shot * HALVES + i)
+            else:
+                finish_handed(kind, i)
     for c in range(9):
         field_out(c).wait()
     for t in range(STEPS):
@@ -441,7 +466,8 @@
             pltpu.VMEM((rounds, ROWS, cols), f32),
             dma((parts,)), dma((4,)), dma((parts,)), dma((STEPS,)),
             dma((parts,)), dma((parts,)), dma((parts,)), dma((parts,)),
-            dma((2 * HALVES, 2)), dma((2 * HALVES, 2)), dma((rounds,)), dma((rounds,)),
+            dma((2 * HALVES, 2)), dma((2 * HALVES, 2)),
+            dma((HALVES, 2)), dma((HALVES, 2)), dma((rounds,)), dma((rounds,)),
         ],
         compiler_params=pltpu.CompilerParams(
             collective_id=0, has_side_effects=True, vmem_limit_bytes=67043328

time: 65.4 us -> 60.8 us (0.930)
  Pallas kernels: 58 us -> 53.3 us
    pallas_call x1, Pallas kernels: 58 us -> 53.3 us  [per_device(): pl.pallas_call(kernel, out_shape=(jax.ShapeDtypeStruct(wavefield.shape, f...]
where the time goes in v3:
time: 60.8 us; the launch traced here: 60.6 us
  Pallas kernels  53.3 us (88%)
  local copies, waits for them, and re-layouts  6.6 us (11%)
  between operations  0.64 us (1%)
    pallas_call x1, Pallas kernels, per_device(): pl.pallas_call(kernel, out_shape=(jax.ShapeDtypeStruct(wavefield.shape, f...  53.3 us
    unnamed x4, local copies, waits for them, and re-layouts  5.31 us
    pallas_call x1, local copies, waits for them, and re-layouts, per_device(): pl.pallas_call(kernel, out_shape=(jax.ShapeDtypeStruct(wavefield.shape, f...  1.3 us

profile of v3, /device:TPU:0, one launch (start us, length us, event | category | flops | bytes accessed | tf_op | source)
XLA Modules:
  0.0 60.6 jit_solution(16140810184979543312)
XLA Ops:
  0.6 53.3 %two_shots.1 = (f32[1,9,8,64,128]{4,3,2,1,0:T(8,128)}, bf16[1,3,9,8,64,128]{5,4,3,2,1,0:T(8,128)(2,1)}, f32[1,3,2]{2,1,0:T(4,128)}) custom-call(f32[1,9,8,64,128]{4,3,2,1,0:T(8,128)} %wave.1, f32[8,64,128]{2,1,0:T(8,128)} %buoy_in.1, f32[8,64,128]{2,1,0:T(8,128)} %lam_in.1, f32[8,64,128]{2,1,0:T(8,128)} %mu_in.1, s32[9,1,8,16]{3,2,1,0:T(8,128)} %exps_in.1, ...), custom_call_target="tpu_custom_call" | custom-call | tf_op jit(solution)/shard_map/two_shots/pallas_call | solution.py:441
  54.0 1.3 %copy.10 = f32[1,3,2]{1,2,0:T(2,128)} copy(f32[1,3,2]{2,1,0:T(4,128)} %get-tuple-element.5) | data formatting | bytes 48 | tf_op jit(solution)/shard_map/two_shots/pallas_call | solution.py:441
  55.3 0.0 copy-start
  55.3 3.5 %copy.13 = f32[1,9,8,64,128]{4,3,2,1,0:T(8,128)} copy(f32[1,9,8,64,128]{4,3,2,1,0:T(8,128)} %get-tuple-element.9) | data formatting | bytes 4718592
  58.8 0.0 copy-done
  58.8 1.8 %copy.14 = bf16[1,3,9,8,64,128]{5,4,3,2,1,0:T(8,128)(2,1)} copy(bf16[1,3,9,8,64,128]{5,4,3,2,1,0:T(8,128)(2,1)S(1)} %copy-done) | data formatting | bytes 7077888
Async XLA Ops:
  55.3 3.5 %copy-start = (bf16[1,3,9,8,64,128]{5,4,3,2,1,0:T(8,128)(2,1)S(1)}, bf16[1,3,9,8,64,128]{5,4,3,2,1,0:T(8,128)(2,1)}, u32[]{:S(2)}) copy-start(bf16[1,3,9,8,64,128]{5,4,3,2,1,0:T(8,128)(2,1)} %get-tuple-element.10) | copy-start | bytes 10616836
